TPU v7x, 32 devices: a whole 2x2x4 slice. The times are simulated.
32 devices in a mesh: grid: 8 (over y, x, core), band: 4 (over z).
Axes of the slice: x: 2, y: 2, z: 4, core: 2. Of those that a mesh axis runs over, the one named last changes fastest.
Arguments:
- start: float32 [1, 4, 1, 64, 32768], P(None, None, None, 'band', 'grid'), may hold values from -6 to 6
- energies: float32 [4, 64, 32768], P(None, 'band', 'grid'), may hold values from -4 to 4
- sites: int32 [3, 1], replicated, may hold values from 0 to 31
- potential: float32 [32, 32, 32], replicated, may hold values from -4 to 400
Outputs:
- alphas: float32 [1, 1, 4], replicated
- betas: float32 [1, 1, 4], replicated
- lanczos: float32 [1, 4, 1, 64, 32768], P(None, None, None, 'band', 'grid')
All inputs are finite; a program needn't handle non-finite values.
Results may differ from a plain program's by a relative error of at most 0.0003.
Values sent between devices are 32-bit elements; how exact they have to be, the bound alone decides.
A program may use at most 64 MiB of HBM per device.

v0:
```python
import functools
import math

import jax
import jax.numpy as jnp
import numpy as np
from jax import lax
from jax.experimental import pallas as pl
from jax.experimental.pallas import tpu as pltpu
from jax.sharding import PartitionSpec as P

ITERS = 4


precise_mode = lax.Precision.HIGHEST


def cas_table(grid_size):
    cells = jnp.arange(grid_size, dtype=jnp.int32)
    phase = cells[:, None] * cells[None, :] % grid_size
    angle = phase.astype(jnp.float32) * (2.0 * math.pi / grid_size)
    return jnp.cos(angle) + jnp.sin(angle)


def shift_axis(field_part, offset, axis_number):
    length = field_part.shape[axis_number]
    doubled = jnp.concatenate([field_part, field_part], axis=axis_number)
    first_index = (length - offset) % length
    return lax.dynamic_slice_in_dim(doubled, first_index, length, axis_number)


def expand_coef(values):
    return values[:, None, :, None, None]


def plane_body(start, energies, sites, potential):
    grid_size = potential.shape[0]
    volume = grid_size * grid_size * grid_size
    atom_count, core_count, pol_count, band_local, kpoint_local = start.shape
    plane_count = grid_size // lax.axis_size("grid")
    position = lax.axis_index("grid")
    chain_count = core_count * pol_count * band_local
    field_count = atom_count * chain_count
    total_count = (
        core_count * band_local * lax.axis_size("band") * kpoint_local * lax.axis_size("grid")
    )
    cas_grid = cas_table(grid_size)
    shifted = shift_axis(potential, sites[0, 0], 0)
    shifted = shift_axis(shifted, sites[1, 0], 1)
    shifted = shift_axis(shifted, sites[2, 0], 2)
    tables = [shifted]
    shifted_all = jnp.stack(tables, axis=-1)
    slab_table = lax.dynamic_slice_in_dim(shifted_all, position * plane_count, plane_count, 1)

    def moment(left, right):
        return jnp.sum(left * right, axis=(1, 3, 4)) / total_count

    start_sum = lax.psum(moment(start, start), ("grid", "band"))
    lanczos = start / expand_coef(jnp.sqrt(start_sum))
    previous = jnp.zeros_like(start)
    beta_prev = jnp.zeros((atom_count, pol_count), jnp.float32)
    alpha_list = []
    beta_list = []
    for iteration in range(ITERS):
        spread_fields = lanczos.reshape(atom_count, chain_count, plane_count, grid_size, grid_size)
        spread_over_z = jnp.einsum(
            "arpyz,wz->pywar", spread_fields, cas_grid, precision=precise_mode
        )
        spread_over_y = jnp.einsum(
            "pywar,uy->puwar", spread_over_z, cas_grid, precision=precise_mode
        )
        direct_spectrum = lax.all_to_all(
            spread_over_y.reshape(plane_count, grid_size, grid_size, field_count),
            "grid",
            split_axis=1,
            concat_axis=0,
            tiled=True,
        )
        field_shape = direct_spectrum.shape
        over_x = jnp.einsum("xvwf,tx->tvwf", direct_spectrum, cas_grid, precision=precise_mode)
        split_view = over_x.reshape(
            field_shape[0], field_shape[1], field_shape[2], atom_count, chain_count
        )
        scaled = split_view * slab_table[..., None]
        back_x = jnp.einsum("tvwar,xt->xvwar", scaled, cas_grid, precision=precise_mode)
        weighted = back_x.reshape(field_shape)
        direct_returned = lax.all_to_all(weighted, "grid", split_axis=0, concat_axis=1, tiled=True)
        fields = direct_returned.reshape(plane_count, grid_size, grid_size, atom_count, chain_count)
        over_z = jnp.einsum("pvwar,zw->pvzar", fields, cas_grid, precision=precise_mode)
        over_y = jnp.einsum("pvzar,yv->arpyz", over_z, cas_grid, precision=precise_mode)
        applied = energies[None, :, None] * lanczos - over_y.reshape(start.shape) / volume
        moments_all = lax.psum(
            (
                moment(lanczos, applied),
                moment(applied, applied),
                moment(lanczos, lanczos),
                moment(previous, previous),
                moment(previous, applied),
                moment(lanczos, previous),
            ),
            ("grid", "band"),
        )
        alpha_now = moments_all[0]
        square = (
            moments_all[1]
            + alpha_now * alpha_now * moments_all[2]
            + beta_prev * beta_prev * moments_all[3]
        )
        square = square - 2.0 * alpha_now * moments_all[0] - 2.0 * beta_prev * moments_all[4]
        square = square + 2.0 * alpha_now * beta_prev * moments_all[5]
        beta_now = jnp.sqrt(square)
        remainder = applied - expand_coef(alpha_now) * lanczos - expand_coef(beta_prev) * previous
        previous = lanczos
        lanczos = remainder / expand_coef(beta_now)
        beta_prev = beta_now
        alpha_list.append(alpha_now)
        beta_list.append(beta_now)
    return (jnp.stack(alpha_list, axis=2), jnp.stack(beta_list, axis=2), lanczos)


MESH = pl.DeviceIdType.MESH
LANES = 128
SUBLANES = 8
GROUPS = 2
PART = SUBLANES // GROUPS


def split(value):
    high = value.astype(jnp.bfloat16)
    return high, (value - high.astype(jnp.float32)).astype(jnp.bfloat16)


def dot3(left, right):
    left_high, left_low = left
    right_high, right_low = right
    left = jnp.concatenate([left_high, left_low, left_high], axis=1)
    right = jnp.concatenate([right_high, right_high, right_low], axis=0)
    return jnp.dot(left, right, preferred_element_type=jnp.float32)


def shifted_potential(table, sites, grid_size):
    cells = grid_size * grid_size
    lane = lax.broadcasted_iota(jnp.int32, table.shape, 1) % grid_size
    for axis in range(3):
        step = 1
        while step < grid_size:
            if axis == 0:
                moved = pltpu.roll(table, step, 0)
            elif axis == 1:
                moved = pltpu.roll(table, step * grid_size, 1)
            else:
                moved = jnp.where(
                    lane >= step,
                    pltpu.roll(table, step, 1),
                    pltpu.roll(table, cells - grid_size + step, 1),
                )
            flag = jnp.full(table.shape, sites[axis] // step % 2, jnp.int32)
            table = jnp.where(flag == 1, moved, table)
            step *= 2
    return table


def total_of(parts):
    total = parts[0]
    for part in parts[1:]:
        total = total + part
    return jnp.sum(jnp.sum(total, axis=0, keepdims=True), axis=1, keepdims=True)


def inverse_of(value):
    return jnp.where(value > 0.0, 1.0 / jnp.where(value > 0.0, value, 1.0), 0.0)


def frequency_order(grid_size):
    cells = np.arange(grid_size)
    return np.concatenate([cells[0::4], cells[2::4], cells[1::2]])


def recursion_kernel(
    sizes, start, energies, sites, pot, forward_y, back_y, all_z, x_far,
    land, coef,
    forward_y_here, back_y_here, all_z_here, x_wide, pot_here, pot_flat, pot_order,
    start_here, energy_here, packed, basis, energy, site_table,
    to_high, to_low, from_high, from_low, vec_high, vec_low, mid_high, mid_low,
    outgoing, sums, gathered,
    table_sem, load_sem, send_sem, recv_sem, out_send, out_recv, sum_send, sum_recv,
):
    n, band_n, grid_size, halves = sizes
    me = lax.axis_index("grid")
    rank = lax.axis_index("band") * n + me
    members = n * band_n
    cells = grid_size * grid_size
    planes = grid_size // n
    rows = grid_size * PART
    piece = planes * PART
    quarter = cells // 4
    total_count = float(grid_size * SUBLANES * cells * members)

    load_copies = [
        pltpu.make_async_copy(source, target, load_sem.at[i])
        for i, (source, target) in enumerate(((start, start_here), (energies, energy_here)))
    ]
    table_copies = [
        pltpu.make_async_copy(source, target, table_sem.at[i])
        for i, (source, target) in enumerate((
            (forward_y, forward_y_here), (back_y, back_y_here), (all_z, all_z_here), (x_far, x_wide), (pot, pot_here)))
    ]
    for copy in load_copies + table_copies:
        copy.start()
    barrier = pltpu.get_barrier_semaphore()
    for k in range(1, members):
        peer = (rank + k) % members
        pl.semaphore_signal(barrier, inc=1, device_id={"grid": peer % n, "band": peer // n}, device_id_type=MESH)

    upper = lax.broadcasted_iota(jnp.int32, (SUBLANES, cells), 0) < PART

    def pack(kind):
        def pack_owner(owner, carry):
            at = pl.ds(pl.multiple_of(owner % halves * SUBLANES, SUBLANES), SUBLANES)
            for pair in range(planes // 2):
                first, second = slice(2 * pair * cells, (2 * pair + 1) * cells), slice((2 * pair + 1) * cells, (2 * pair + 2) * cells)
                if kind == 0:
                    one, two = start_here[0, owner // halves, 0, at, first], start_here[0, owner // halves, 0, at, second]
                else:
                    one, two = energy_here[owner // halves, at, first], energy_here[owner // halves, at, second]
                here = slice(pair * SUBLANES, (pair + 1) * SUBLANES)
                packed[kind, 0, owner, here, :] = jnp.where(upper, one, pltpu.roll(two, PART, 0))
                packed[kind, 1, owner, here, :] = jnp.where(upper, pltpu.roll(one, PART, 0), two)
            return carry

        lax.fori_loop(0, n, pack_owner, 0)

    my_rows = pl.ds(pl.multiple_of(me * piece, piece), piece)

    def piece_copy(kind, group, k):
        peer = (me + k) % n
        target = basis.at[group, 0, my_rows, :] if kind == 0 else energy.at[group, my_rows, :]
        return pltpu.make_async_remote_copy(
            src_ref=packed.at[kind, group, peer], dst_ref=target, send_sem=send_sem.at[kind, group, k],
            recv_sem=recv_sem.at[kind, group, k], device_id={"grid": peer}, device_id_type=MESH)

    load_copies[0].wait()
    pack(0)
    load_copies[1].wait()
    pack(1)
    pl.semaphore_wait(barrier, members - 1)
    for group in range(GROUPS):
        for kind in range(2):
            for k in range(1, n):
                piece_copy(kind, group, k).start()
    for group in range(GROUPS):
        basis[group, 0, my_rows, :] = packed[0, group, me]
        energy[group, my_rows, :] = packed[1, group, me]

    for copy in table_copies:
        copy.wait()

    def forward_rows(y, carry):
        high, low = split(forward_y_here[pl.ds(y, 1), :] * all_z_here[...])
        at = pl.ds(pl.multiple_of(y * grid_size, grid_size), grid_size)
        to_high[at, :] = high
        to_low[at, :] = low
        return carry

    def back_rows(v, carry):
        high, low = split(back_y_here[pl.ds(v, 1), :] * all_z_here[:, : 2 * quarter])
        at = pl.ds(pl.multiple_of(v * grid_size, grid_size), grid_size)
        from_high[at, :] = high
        from_low[at, :] = low
        return carry

    lax.fori_loop(0, grid_size // 2, forward_rows, 0)
    lax.fori_loop(0, grid_size, back_rows, 0)
    for y in range(grid_size):
        pot_flat[:, y * grid_size:(y + 1) * grid_size] = pot_here[:, y, :]
    pot_flat[...] = shifted_potential(pot_flat[...], sites, grid_size) * (1.0 / (grid_size * cells))
    for place, v in enumerate(frequency_order(grid_size)):
        pot_order[:, place * grid_size:(place + 1) * grid_size] = pot_flat[:, int(v) * grid_size:(int(v) + 1) * grid_size]
    for x in range(grid_size):
        site_table[PART * x:PART * (x + 1), :] = jnp.broadcast_to(pot_order[x:x + 1, :], (PART, cells))

    quarters = [slice(i * quarter, (i + 1) * quarter) for i in range(4)]
    odd = slice(2 * quarter, 4 * quarter)
    lane = lax.broadcasted_iota(jnp.int32, (1, LANES), 1)
    tall = 2 * SUBLANES

    def lane_is(place):
        return lane == jnp.full((1, LANES), place, jnp.int32)

    def folded(product):
        return sum((product[i:i + SUBLANES] for i in range(SUBLANES, product.shape[0], SUBLANES)), product[:SUBLANES])

    def times_x(value):
        high, low = split(value)
        return jnp.dot(x_wide[...], jnp.concatenate([high, high, low], axis=0), preferred_element_type=jnp.float32)

    def message_copy(stage, k):
        peer = (rank + k) % members
        return pltpu.make_async_remote_copy(
            src_ref=sums.at[stage, rank], dst_ref=sums.at[stage, rank], send_sem=sum_send.at[stage, k],
            recv_sem=sum_recv.at[stage, k], device_id={"grid": peer % n, "band": peer // n}, device_id_type=MESH)

    def send_message(stage, message):
        sums[stage, rank] = message
        for k in range(1, members):
            message_copy(stage, k).start()

    def step(t, carry):
        alpha, gamma, norm_before, message = carry
        group, j = t // ITERS, t % ITERS
        before, earlier = jnp.maximum(j - 1, 0), jnp.maximum(j - 2, 0)

        @pl.when(j == 0)
        def _():
            for k in range(1, n):
                piece_copy(0, group, k).wait_recv()

        norm_parts = []
        for r in range(0, rows, tall):
            at = slice(r, r + tall)
            q = []
            for cols in quarters:
                value = basis[group, j, at, cols] - alpha * basis[group, before, at, cols] - gamma * basis[group, earlier, at, cols]
                basis[group, j, at, cols] = value
                q.append(value)
            norm_parts.append(folded(q[0] * q[0] + q[1] * q[1] + q[2] * q[2] + q[3] * q[3]))
            even, other = q[0] + q[2], q[1] + q[3]
            for cols, value in zip(quarters, (even + other, even - other, q[0] - q[2], q[1] - q[3])):
                vec_high[at, cols], vec_low[at, cols] = split(value)
        for cols, depth in ((quarters[0], quarter), (quarters[1], quarter), (odd, 2 * quarter)):
            spectrum = dot3((vec_high[:, cols], vec_low[:, cols]), (to_high[:depth, cols], to_low[:depth, cols]))
            spectrum = times_x(spectrum) * site_table[:, cols]
            mid_high[:, cols], mid_low[:, cols] = split(times_x(spectrum))
        norm = total_of(norm_parts)

        @pl.when(j == 0)
        def _():
            for k in range(1, n):
                piece_copy(1, group, k).wait_recv()

        def back(at, cols):
            return dot3((mid_high[:, at], mid_low[:, at]), (from_high[at, cols], from_low[at, cols]))

        zero, two = back(quarters[0], slice(0, quarter)), back(quarters[1], slice(0, quarter))
        odds = back(odd, slice(0, 2 * quarter))
        plus, minus = zero + two, zero - two
        one, three = odds[:, :quarter], odds[:, quarter:]
        alpha_parts, square_parts = [], []
        for cols, value in zip(quarters, (plus + one, minus + three, plus - one, minus - three)):
            here = basis[group, j, :, cols]
            new = energy[group, :, cols] * here - value
            basis[group, j + 1, :, cols] = new
            alpha_parts.append(folded(here * new))
            square_parts.append(folded(new * new))
        alpha = total_of(alpha_parts) * inverse_of(norm)
        gamma = jnp.where(jnp.full((1, 1), j, jnp.int32) == 0, 0.0, norm * inverse_of(norm_before))
        norm_after = jnp.maximum(total_of(square_parts) - alpha * alpha * norm - gamma * norm, 0.0)
        place = SUBLANES * group + j
        message = jnp.where(lane_is(place), norm, message)
        message = jnp.where(lane_is(place + 1), norm_after, message)
        message = jnp.where(lane_is(place + LANES // 2), alpha, message)

        @pl.when(t == GROUPS * ITERS - 2)
        def _():
            send_message(0, message)

        keep = jnp.where(jnp.full((1, 1), j, jnp.int32) == ITERS - 1, 0.0, 1.0)
        return alpha * keep, gamma * keep, norm, message

    nothing = jnp.zeros((1, 1), jnp.float32)
    message = lax.fori_loop(0, GROUPS * ITERS, step, (nothing, nothing, nothing, jnp.zeros((1, LANES), jnp.float32)))[3]
    send_message(1, message)

    def tables_of(stage):
        for k in range(1, members):
            message_copy(stage, k).wait_recv()
        for r in range(members):
            gathered[stage, r:r + 1, :] = sums[stage, r]
        table = gathered[stage]
        norms = jnp.where(wide_lane < LANES // 2, table, 0.0)
        return norms, pltpu.roll(table, LANES // 2, 1), jnp.where(order > 0, norms * inverse_of(pltpu.roll(norms, 1, 1)), 0.0)

    wide_lane = lax.broadcasted_iota(jnp.int32, (members, LANES), 1)
    order = wide_lane % SUBLANES
    used = jnp.logical_and(order <= ITERS, wide_lane < SUBLANES * GROUPS)

    def inner(norms, left, right):
        return total_of([norms * left * right]) / total_count

    def global_step(tables, vector, previous, beta):
        norms, diagonal, coupling = tables
        raised = jnp.where(order > 0, pltpu.roll(vector, 1, 1), 0.0)
        lowered = jnp.where(order < ITERS, pltpu.roll(coupling * vector, LANES - 1, 1), 0.0)
        image = jnp.where(used, raised + jnp.where(order < ITERS, diagonal, 0.0) * vector + lowered, 0.0)
        alpha_now = inner(norms, vector, image)
        rest = image - alpha_now * vector - beta * previous
        beta_now = jnp.sqrt(inner(norms, rest, rest))
        return alpha_now, beta_now, rest / beta_now, vector

    alphas, betas = jnp.zeros((1, LANES), jnp.float32), jnp.zeros((1, LANES), jnp.float32)
    tables = tables_of(0)
    first = jnp.where(jnp.logical_and(used, order == 0), 1.0, 0.0)
    vector, previous, beta = first / jnp.sqrt(inner(tables[0], first, first)), jnp.zeros((members, LANES), jnp.float32), nothing
    for j in range(ITERS):
        if j == ITERS - 1:
            tables = tables_of(1)
        alpha, beta, vector, previous = global_step(tables, vector, previous, beta)
        alphas, betas = jnp.where(lane == j, alpha, alphas), jnp.where(lane == j, beta, betas)
    coef[0:1, :] = alphas
    coef[1:2, :] = betas
    norms, diagonal, coupling = tables
    top = ITERS - 1
    weights = vector - jnp.where(order == top, diagonal * pltpu.roll(vector, LANES - 1, 1), 0.0)
    weights = weights - jnp.where(order == top - 1, pltpu.roll(coupling, LANES - 1, 1) * pltpu.roll(vector, LANES - 2, 1), 0.0)
    mine = lax.broadcasted_iota(jnp.int32, (members, LANES), 0) == jnp.full((members, LANES), rank, jnp.int32)
    weights = jnp.sum(jnp.where(mine, weights, 0.0), axis=0, keepdims=True)
    scales = [
        [jnp.sum(jnp.where(lane == SUBLANES * group + i, weights, 0.0), axis=1, keepdims=True) for i in range(ITERS + 1)]
        for group in range(GROUPS)
    ]
    out_copies = []
    for k in range(1, n + 1):
        peer = (me + k) % n
        at = pl.ds(pl.multiple_of(peer * piece, piece), piece)
        for group in range(GROUPS):
            value = sum((scales[group][i] * basis[group, i, at, :] for i in range(1, ITERS + 1)), scales[group][0] * basis[group, 0, at, :])
            if k < n:
                outgoing[peer, group] = value
            else:
                land[me, group] = value
        if k < n:
            copy = pltpu.make_async_remote_copy(
                src_ref=outgoing.at[peer], dst_ref=land.at[me], send_sem=out_send.at[k], recv_sem=out_recv.at[k],
                device_id={"grid": peer}, device_id_type=MESH)
            copy.start()
            out_copies.append(copy)
    for group in range(GROUPS):
        for kind in range(2):
            for k in range(1, n):
                piece_copy(kind, group, k).wait_send()
    for stage in range(2):
        for k in range(1, members):
            message_copy(stage, k).wait_send()
    for copy in out_copies:
        copy.wait()


def unpack_kernel(halves, planes, land, coef, out, alphas, betas):
    owners, cells = land.shape[0], land.shape[3]
    upper = lax.broadcasted_iota(jnp.int32, (SUBLANES, cells), 0) < PART
    for owner in range(owners):
        at = slice(owner % halves * SUBLANES, (owner % halves + 1) * SUBLANES)
        for pair in range(planes // 2):
            here = slice(pair * SUBLANES, (pair + 1) * SUBLANES)
            one, two = land[owner, 0, here, :], land[owner, 1, here, :]
            out[0, owner // halves, 0, at, 2 * pair * cells:(2 * pair + 1) * cells] = jnp.where(upper, one, pltpu.roll(two, PART, 0))
            out[0, owner // halves, 0, at, (2 * pair + 1) * cells:(2 * pair + 2) * cells] = jnp.where(upper, pltpu.roll(one, PART, 0), two)
    alphas[0] = coef[0:1, :ITERS]
    betas[0] = coef[1:2, :ITERS]


def field_body(start, energies, sites, potential):
    grid_size = potential.shape[0]
    cells = grid_size * grid_size
    n, band_n = lax.axis_size("grid"), lax.axis_size("band")
    halves = start.shape[3] // SUBLANES
    planes = grid_size // n
    rows, piece, half_cells = grid_size * PART, planes * PART, cells // 2
    index = np.arange(grid_size)
    angle = (index[:, None] * index[None, :] % grid_size) * (2.0 * math.pi / grid_size)
    cas = np.cos(angle) + np.sin(angle)
    ordered = cas[frequency_order(grid_size)]
    half_grid = grid_size // 2
    forward_y = jnp.asarray(np.repeat(ordered.T[:half_grid], grid_size, axis=1), jnp.float32)
    back_y = jnp.asarray(np.repeat(ordered[:, :half_grid], grid_size, axis=1), jnp.float32)
    all_z = jnp.asarray(np.tile(cas, (1, grid_size)), jnp.float32)
    x_wide = np.kron(cas, np.eye(PART)).astype(np.float32)
    x_high = x_wide.astype(jnp.bfloat16)
    x_low = (x_wide - x_high.astype(np.float32)).astype(jnp.bfloat16)
    x_wide = jnp.asarray(np.concatenate([x_high, x_low, x_high], axis=1))
    vmem = pl.BlockSpec(memory_space=pltpu.VMEM)
    hbm = pl.BlockSpec(memory_space=pltpu.MemorySpace.HBM)
    f32, bf16 = jnp.float32, jnp.bfloat16
    dma = pltpu.SemaphoreType.DMA
    members = n * band_n
    land_shape = (n, GROUPS, piece, cells)
    start, energies, potential = (pltpu.with_memory_space_constraint(value, pltpu.MemorySpace.HBM) for value in (start, energies, potential))
    land, coef = pl.pallas_call(
        functools.partial(recursion_kernel, (n, band_n, grid_size, halves)),
        out_shape=(jax.ShapeDtypeStruct(land_shape, f32), jax.ShapeDtypeStruct((2, LANES), f32)),
        in_specs=[hbm, hbm, pl.BlockSpec(memory_space=pltpu.SMEM)] + [hbm] * 5,
        out_specs=(vmem, vmem),
        scratch_shapes=[
            pltpu.VMEM((half_grid, cells), f32), pltpu.VMEM((grid_size, half_cells), f32), pltpu.VMEM((grid_size, cells), f32),
            pltpu.VMEM((rows, 3 * rows), bf16), pltpu.VMEM(potential.shape, f32),
            pltpu.VMEM((grid_size, cells), f32), pltpu.VMEM((grid_size, cells), f32),
            pltpu.VMEM(start.shape, f32), pltpu.VMEM(energies.shape, f32),
            pltpu.VMEM((2, GROUPS, n, piece, cells), f32),
            pltpu.VMEM((GROUPS, ITERS + 1, rows, cells), f32), pltpu.VMEM((GROUPS, rows, cells), f32),
            pltpu.VMEM((rows, cells), f32),
            pltpu.VMEM((half_cells, cells), bf16), pltpu.VMEM((half_cells, cells), bf16),
            pltpu.VMEM((cells, half_cells), bf16), pltpu.VMEM((cells, half_cells), bf16),
            pltpu.VMEM((rows, cells), bf16), pltpu.VMEM((rows, cells), bf16),
            pltpu.VMEM((rows, cells), bf16), pltpu.VMEM((rows, cells), bf16),
            pltpu.VMEM(land_shape, f32),
            pltpu.VMEM((2, members, 1, LANES), f32), pltpu.VMEM((2, members, LANES), f32),
            dma((5,)), dma((2,)), dma((2, GROUPS, n)), dma((2, GROUPS, n)), dma((n,)), dma((n,)),
            dma((2, members)), dma((2, members)),
        ],
        compiler_params=pltpu.CompilerParams(collective_id=0, has_side_effects=True, vmem_limit_bytes=36 * 1024 * 1024),
    )(start, energies, sites[:, 0], potential, *(pltpu.with_memory_space_constraint(value, pltpu.MemorySpace.HBM) for value in (forward_y, back_y, all_z, x_wide)))
    scalar = jax.ShapeDtypeStruct((1, 1, ITERS), f32)
    out, alphas, betas = pl.pallas_call(
        functools.partial(unpack_kernel, halves, planes),
        out_shape=(jax.ShapeDtypeStruct(start.shape, f32), scalar, scalar),
        in_specs=[vmem, vmem],
        out_specs=(vmem, vmem, vmem),
        compiler_params=pltpu.CompilerParams(vmem_limit_bytes=8 * 1024 * 1024),
    )(land, coef)
    return alphas, betas, out


def body(start, energies, sites, potential):
    atoms, cores, pols, bands, _ = start.shape
    grid_size = potential.shape[0]
    n = lax.axis_size("grid")
    whole_fields = (
        atoms == 1 and pols == 1 and bands % SUBLANES == 0 and cores * bands == SUBLANES * n
        and grid_size % (2 * SUBLANES) == 0 and grid_size % (2 * n) == 0
        and grid_size * grid_size % (4 * LANES) == 0 and n * lax.axis_size("band") % SUBLANES == 0
    )
    return (field_body if whole_fields else plane_body)(start, energies, sites, potential)


def solution(mesh):
    in_specs = (P(None, None, None, "band", "grid"), P(None, "band", "grid"), P(), P())
    out_specs = (P(), P(), P(None, None, None, "band", "grid"))
    return jax.shard_map(body, mesh=mesh, in_specs=in_specs, out_specs=out_specs, check_vma=False)
```

profile of v0, /device:TPU:1, one launch (start us, length us, event | category | flops | bytes accessed | tf_op | source)
XLA Modules:
  0.0 60.0 jit_solution(2652296840490824058)
XLA Ops:
  0.6 0.0 copy-start
  0.6 0.6 %copy-done = s32[3,1]{0,1:T(1,128)S(1)} copy-done((s32[3,1]{0,1:T(1,128)S(1)}, s32[3,1]{0,1:T(1,128)}, u32[]{:S(2)}) %copy-start) | copy-done | bytes 36
  1.3 57.6 %shard_map.103 = (f32[8,2,16,1024]{3,2,1,0:T(8,128)S(1)}, f32[2,128]{1,0:T(2,128)S(1)}) custom-call(f32[1,4,1,16,4096]{4,3,2,1,0:T(8,128)} %start.1, f32[4,16,4096]{2,1,0:T(8,128)} %energies.1, s32[3]{0:T(128)S(1)} %bitcast.1, f32[32,32,32]{2,1,0:T(8,128)} %pot.1, f32[16,1024]{1,0:T(8,128)} %constant.8.clone.forward_y, f32[32,512]{1,0:T(8,128)} %constant.9.clone.back_y, ...), custom_call_target="tpu_custom_call" | custom-call | tf_op jit(solution)/shard_map/pallas_call | solution.py:488
  58.9 1.0 %shard_map.104 = (f32[1,4,1,16,4096]{4,3,2,1,0:T(8,128)}, f32[1,1,4]{2,1,0:T(1,128)}, f32[1,1,4]{2,1,0:T(1,128)}) custom-call(f32[8,2,16,1024]{3,2,1,0:T(8,128)S(1)} %get-tuple-element.8.land, f32[2,128]{1,0:T(2,128)S(1)} %get-tuple-element.9.coef), custom_call_target="tpu_custom_call" | custom-call | tf_op jit(solution)/shard_map/pallas_call | solution.py:513
Async XLA Ops:
  0.6 0.7 %copy-start = (s32[3,1]{0,1:T(1,128)S(1)}, s32[3,1]{0,1:T(1,128)}, u32[]{:S(2)}) copy-start(s32[3,1]{0,1:T(1,128)} %param.10) | copy-start | bytes 40
where the time goes:
time: 60.1 us; the launch traced here: 60 us
  Pallas kernels  58.7 us (98%)
  local copies, waits for them, and re-layouts  0.65 us (1%)
  between operations  0.65 us (1%)
    pallas_call x1, Pallas kernels, field_body(): pl.pallas_call(functools.partial(recursion_kernel, (n, band_n, grid_size,...  57.6 us

commit v1 on v0

--- a/solution.py
+++ b/solution.py
@@ -122,6 +122,8 @@
 LANES = 128
 SUBLANES = 8
 GROUPS = 2
+EARLY = 1
+FIRST_EIGHTHS = 5
 PART = SUBLANES // GROUPS
 
 
@@ -179,20 +181,22 @@
 def recursion_kernel(
     sizes, start, energies, sites, pot, forward_y, back_y, all_z, x_far,
     land, coef,
-    forward_y_here, back_y_here, all_z_here, x_wide, pot_here, pot_flat, pot_order,
+    sites_here, forward_y_here, back_y_here, all_z_here, x_wide, pot_here, pot_flat, pot_order,
     start_here, energy_here, packed, basis, energy, site_table,
-    to_high, to_low, from_high, from_low, vec_high, vec_low, mid_high, mid_low,
-    outgoing, sums, gathered,
-    table_sem, load_sem, send_sem, recv_sem, out_send, out_recv, sum_send, sum_recv,
+    to_high, to_low, from_high, from_low, vec_high, vec_low, mid_high, mid_low, past,
+    outgoing, early_land, sums, gathered,
+    table_sem, load_sem, send_sem, recv_sem, out_send, out_recv, sum_send, sum_recv, plane_sem, early_send, early_recv,
 ):
     n, band_n, grid_size, halves = sizes
     me = lax.axis_index("grid")
-    rank = lax.axis_index("band") * n + me
+    band = lax.axis_index("band")
+    rank = band * n + me
     members = n * band_n
     cells = grid_size * grid_size
     planes = grid_size // n
     rows = grid_size * PART
     piece = planes * PART
+    early = EARLY * piece // 2
     quarter = cells // 4
     total_count = float(grid_size * SUBLANES * cells * members)
 
@@ -203,14 +207,15 @@
     table_copies = [
         pltpu.make_async_copy(source, target, table_sem.at[i])
         for i, (source, target) in enumerate((
-            (forward_y, forward_y_here), (back_y, back_y_here), (all_z, all_z_here), (x_far, x_wide), (pot, pot_here)))
+            (forward_y, forward_y_here), (back_y, back_y_here), (all_z, all_z_here), (x_far, x_wide), (pot, pot_here), (sites, sites_here)))
     ]
     for copy in load_copies + table_copies:
         copy.start()
     barrier = pltpu.get_barrier_semaphore()
-    for k in range(1, members):
-        peer = (rank + k) % members
-        pl.semaphore_signal(barrier, inc=1, device_id={"grid": peer % n, "band": peer // n}, device_id_type=MESH)
+    for k in range(1, band_n):
+        pl.semaphore_signal(barrier, inc=1, device_id={"band": (band + k) % band_n}, device_id_type=MESH)
+    for k in range(1, n):
+        pl.semaphore_signal(barrier, inc=1, device_id={"grid": (me + k) % n}, device_id_type=MESH)
 
     upper = lax.broadcasted_iota(jnp.int32, (SUBLANES, cells), 0) < PART
 
@@ -243,11 +248,13 @@
     pack(0)
     load_copies[1].wait()
     pack(1)
-    pl.semaphore_wait(barrier, members - 1)
+    pl.semaphore_wait(barrier, n + band_n - 2)
     for group in range(GROUPS):
         for kind in range(2):
             for k in range(1, n):
                 piece_copy(kind, group, k).start()
+    for k in range(1, band_n):
+        pl.semaphore_signal(plane_sem, inc=1, device_id={"band": (band + k) % band_n}, device_id_type=MESH)
     for group in range(GROUPS):
         basis[group, 0, my_rows, :] = packed[0, group, me]
         energy[group, my_rows, :] = packed[1, group, me]
@@ -273,12 +280,15 @@
     lax.fori_loop(0, grid_size, back_rows, 0)
     for y in range(grid_size):
         pot_flat[:, y * grid_size:(y + 1) * grid_size] = pot_here[:, y, :]
-    pot_flat[...] = shifted_potential(pot_flat[...], sites, grid_size) * (1.0 / (grid_size * cells))
+    pot_flat[...] = shifted_potential(pot_flat[...], sites_here, grid_size) * (1.0 / (grid_size * cells))
     for place, v in enumerate(frequency_order(grid_size)):
         pot_order[:, place * grid_size:(place + 1) * grid_size] = pot_flat[:, int(v) * grid_size:(int(v) + 1) * grid_size]
     for x in range(grid_size):
         site_table[PART * x:PART * (x + 1), :] = jnp.broadcast_to(pot_order[x:x + 1, :], (PART, cells))
 
+    past[...] = jnp.zeros_like(past)
+    pl.semaphore_wait(plane_sem, band_n - 1)
+
     quarters = [slice(i * quarter, (i + 1) * quarter) for i in range(4)]
     odd = slice(2 * quarter, 4 * quarter)
     lane = lax.broadcasted_iota(jnp.int32, (1, LANES), 1)
@@ -294,82 +304,135 @@
         high, low = split(value)
         return jnp.dot(x_wide[...], jnp.concatenate([high, high, low], axis=0), preferred_element_type=jnp.float32)
 
+    first_columns = cells * FIRST_EIGHTHS // 8
+    early_columns = (pl.ds(0, first_columns), pl.ds(first_columns, cells - first_columns))
+
+    def early_copy(part, k):
+        peer = (me + k) % n
+        at = pl.ds(pl.multiple_of(peer * piece, SUBLANES), early)
+        return pltpu.make_async_remote_copy(
+            src_ref=basis.at[0, pl.ds(1, ITERS), at, early_columns[part]], dst_ref=early_land.at[me, :, :, early_columns[part]],
+            send_sem=early_send.at[part, k], recv_sem=early_recv.at[part, k], device_id={"grid": peer}, device_id_type=MESH)
+
     def message_copy(stage, k):
-        peer = (rank + k) % members
         return pltpu.make_async_remote_copy(
-            src_ref=sums.at[stage, rank], dst_ref=sums.at[stage, rank], send_sem=sum_send.at[stage, k],
-            recv_sem=sum_recv.at[stage, k], device_id={"grid": peer % n, "band": peer // n}, device_id_type=MESH)
+            src_ref=sums.at[stage, rank], dst_ref=sums.at[stage, rank], send_sem=sum_send.at[stage, k], recv_sem=sum_recv.at[stage, k],
+            device_id={"grid": (me + k % n) % n, "band": (band + k // n) % band_n}, device_id_type=MESH)
+
+    far_first = sorted(range(1, members), key=lambda k: -min(k // n, band_n - k // n))
 
     def send_message(stage, message):
         sums[stage, rank] = message
-        for k in range(1, members):
+        for k in far_first:
             message_copy(stage, k).start()
 
-    def step(t, carry):
-        alpha, gamma, norm_before, message = carry
+    tiles = [slice(r, r + tall) for r in range(0, rows, tall)]
+
+    def spread_quarters(at, q):
+        even, other = q[0] + q[2], q[1] + q[3]
+        for cols, value in zip(quarters, (even + other, even - other, q[0] - q[2], q[1] - q[3])):
+            vec_high[at, cols], vec_low[at, cols] = split(value)
+
+    def settle(t, results):
+        alpha_part, square_part, norm, norm_before, message = results
+        j = (t + ITERS - 1) % ITERS
+        alpha = total_of([alpha_part]) * inverse_of(norm)
+        gamma = jnp.where(jnp.full((1, 1), j, jnp.int32) == 0, 0.0, norm * inverse_of(norm_before))
+        norm_after = jnp.maximum(total_of([square_part]) - alpha * alpha * norm - gamma * norm, 0.0)
+        place = SUBLANES * ((t + ITERS - 1) // ITERS - 1) + j
+        message = jnp.where(lane_is(place), norm, message)
+        message = jnp.where(lane_is(place + 1), norm_after, message)
+        message = jnp.where(lane_is(place + LANES // 2), alpha, message)
+        return alpha, gamma, message
+
+    def step(t, results, final=False):
+        alpha, gamma, message = settle(t, results)
         group, j = t // ITERS, t % ITERS
-        before, earlier = jnp.maximum(j - 1, 0), jnp.maximum(j - 2, 0)
-
-        @pl.when(j == 0)
-        def _():
-            for k in range(1, n):
-                piece_copy(0, group, k).wait_recv()
-
-        norm_parts = []
-        for r in range(0, rows, tall):
-            at = slice(r, r + tall)
-            q = []
+        before, earlier, now = jnp.maximum(j - 1, 0), jnp.maximum(j - 2, 0), j % 2
+        if final:
+            send_message(0, message)
+        else:
+            keep = jnp.where(jnp.full((1, 1), j, jnp.int32) == 0, 0.0, 1.0)
+            alpha, gamma = alpha * keep, gamma * keep
+
+            @pl.when(j == 0)
+            def _():
+                for k in range(1, n):
+                    piece_copy(0, group, k).wait_recv()
+                for at in tiles:
+                    spread_quarters(at, [basis[group, 0, at, cols] for cols in quarters])
+
+        def forward(i):
+            cols = quarters[i]
+            source, depth = (cols, quarter) if i < 2 else (odd, 2 * quarter)
+            spectrum = dot3((vec_high[:, source], vec_low[:, source]), (to_high[:depth, cols], to_low[:depth, cols]))
+            spectrum = spectrum - alpha * past[1 - now, :, cols] - gamma * past[now, :, cols]
+            past[now, :, cols] = spectrum
+            return spectrum
+
+        def weigh(i, spectrum):
+            return times_x(spectrum) * site_table[:, quarters[i]]
+
+        def finish(i, spectrum):
+            mid_high[:, quarters[i]], mid_low[:, quarters[i]] = split(times_x(spectrum))
+
+        first, second = forward(0), forward(1)
+        first = weigh(0, first)
+        third = forward(2)
+        second = weigh(1, second)
+        finish(0, first)
+        fourth = forward(3)
+        third = weigh(2, third)
+        finish(1, second)
+        fourth = weigh(3, fourth)
+        finish(2, third)
+        finish(3, fourth)
+        norm_part = jnp.zeros((SUBLANES, quarter), jnp.float32)
+        for at in tiles:
             for cols in quarters:
                 value = basis[group, j, at, cols] - alpha * basis[group, before, at, cols] - gamma * basis[group, earlier, at, cols]
                 basis[group, j, at, cols] = value
-                q.append(value)
-            norm_parts.append(folded(q[0] * q[0] + q[1] * q[1] + q[2] * q[2] + q[3] * q[3]))
-            even, other = q[0] + q[2], q[1] + q[3]
-            for cols, value in zip(quarters, (even + other, even - other, q[0] - q[2], q[1] - q[3])):
-                vec_high[at, cols], vec_low[at, cols] = split(value)
-        for cols, depth in ((quarters[0], quarter), (quarters[1], quarter), (odd, 2 * quarter)):
-            spectrum = dot3((vec_high[:, cols], vec_low[:, cols]), (to_high[:depth, cols], to_low[:depth, cols]))
-            spectrum = times_x(spectrum) * site_table[:, cols]
-            mid_high[:, cols], mid_low[:, cols] = split(times_x(spectrum))
-        norm = total_of(norm_parts)
-
-        @pl.when(j == 0)
-        def _():
-            for k in range(1, n):
-                piece_copy(1, group, k).wait_recv()
+                norm_part = norm_part + folded(value * value)
+        norm = total_of([norm_part])
+        if not final:
+
+            @pl.when(j == 0)
+            def _():
+                for k in range(1, n):
+                    piece_copy(1, group, k).wait_recv()
+
+            @pl.when(t == ITERS)
+            def _():
+                for k in range(1, n):
+                    early_copy(0, k).start()
 
         def back(at, cols):
             return dot3((mid_high[:, at], mid_low[:, at]), (from_high[at, cols], from_low[at, cols]))
 
         zero, two = back(quarters[0], slice(0, quarter)), back(quarters[1], slice(0, quarter))
         odds = back(odd, slice(0, 2 * quarter))
-        plus, minus = zero + two, zero - two
-        one, three = odds[:, :quarter], odds[:, quarter:]
-        alpha_parts, square_parts = [], []
-        for cols, value in zip(quarters, (plus + one, minus + three, plus - one, minus - three)):
-            here = basis[group, j, :, cols]
-            new = energy[group, :, cols] * here - value
-            basis[group, j + 1, :, cols] = new
-            alpha_parts.append(folded(here * new))
-            square_parts.append(folded(new * new))
-        alpha = total_of(alpha_parts) * inverse_of(norm)
-        gamma = jnp.where(jnp.full((1, 1), j, jnp.int32) == 0, 0.0, norm * inverse_of(norm_before))
-        norm_after = jnp.maximum(total_of(square_parts) - alpha * alpha * norm - gamma * norm, 0.0)
-        place = SUBLANES * group + j
-        message = jnp.where(lane_is(place), norm, message)
-        message = jnp.where(lane_is(place + 1), norm_after, message)
-        message = jnp.where(lane_is(place + LANES // 2), alpha, message)
-
-        @pl.when(t == GROUPS * ITERS - 2)
-        def _():
-            send_message(0, message)
-
-        keep = jnp.where(jnp.full((1, 1), j, jnp.int32) == ITERS - 1, 0.0, 1.0)
-        return alpha * keep, gamma * keep, norm, message
-
-    nothing = jnp.zeros((1, 1), jnp.float32)
-    message = lax.fori_loop(0, GROUPS * ITERS, step, (nothing, nothing, nothing, jnp.zeros((1, LANES), jnp.float32)))[3]
-    send_message(1, message)
+        alpha_part, square_part = jnp.zeros((SUBLANES, quarter), jnp.float32), jnp.zeros((SUBLANES, quarter), jnp.float32)
+        for at in tiles:
+            plus, minus, one, three = zero[at] + two[at], zero[at] - two[at], odds[at, :quarter], odds[at, quarter:]
+            q = []
+            for cols, value in zip(quarters, (plus + one, minus + three, plus - one, minus - three)):
+                here = basis[group, j, at, cols]
+                new = energy[group, at, cols] * here - value
+                basis[group, j + 1, at, cols] = new
+                alpha_part = alpha_part + folded(here * new)
+                square_part = square_part + folded(new * new)
+                q.append(new)
+            if not final:
+                spread_quarters(at, q)
+        return alpha_part, square_part, norm, results[2], message
+
+    nothing, no_part = jnp.zeros((1, 1), jnp.float32), jnp.zeros((SUBLANES, quarter), jnp.float32)
+    results = (no_part, no_part, nothing, nothing, jnp.zeros((1, LANES), jnp.float32))
+    steps = GROUPS * ITERS
+    results = step(steps - 1, lax.fori_loop(0, steps - 1, step, results), True)
+    send_message(1, settle(steps, results)[2])
+    for k in range(1, n):
+        early_copy(1, k).start()
 
     def tables_of(stage):
         for k in range(1, members):
@@ -412,28 +475,44 @@
     top = ITERS - 1
     weights = vector - jnp.where(order == top, diagonal * pltpu.roll(vector, LANES - 1, 1), 0.0)
     weights = weights - jnp.where(order == top - 1, pltpu.roll(coupling, LANES - 1, 1) * pltpu.roll(vector, LANES - 2, 1), 0.0)
-    mine = lax.broadcasted_iota(jnp.int32, (members, LANES), 0) == jnp.full((members, LANES), rank, jnp.int32)
-    weights = jnp.sum(jnp.where(mine, weights, 0.0), axis=0, keepdims=True)
-    scales = [
-        [jnp.sum(jnp.where(lane == SUBLANES * group + i, weights, 0.0), axis=1, keepdims=True) for i in range(ITERS + 1)]
-        for group in range(GROUPS)
-    ]
+    gathered[2] = weights
+
+    def scales_of(owner):
+        row = gathered[2, pl.ds(owner, 1), :]
+        return [
+            [jnp.sum(jnp.where(lane == SUBLANES * group + i, row, 0.0), axis=1, keepdims=True) for i in range(ITERS + 1)]
+            for group in range(GROUPS)
+        ]
+
+    scales = scales_of(rank)
     out_copies = []
     for k in range(1, n + 1):
         peer = (me + k) % n
-        at = pl.ds(pl.multiple_of(peer * piece, piece), piece)
         for group in range(GROUPS):
+            skip = early if group == 0 and k < n else 0
+            at = pl.ds(pl.multiple_of(peer * piece + skip, SUBLANES), piece - skip)
             value = sum((scales[group][i] * basis[group, i, at, :] for i in range(1, ITERS + 1)), scales[group][0] * basis[group, 0, at, :])
+            target = slice(group * piece + skip, (group + 1) * piece)
             if k < n:
-                outgoing[peer, group] = value
+                outgoing[peer, target, :] = value
             else:
-                land[me, group] = value
+                land[me, target, :] = value
         if k < n:
+            sent = pl.ds(early, GROUPS * piece - early)
             copy = pltpu.make_async_remote_copy(
-                src_ref=outgoing.at[peer], dst_ref=land.at[me], send_sem=out_send.at[k], recv_sem=out_recv.at[k],
+                src_ref=outgoing.at[peer, sent, :], dst_ref=land.at[me, sent, :], send_sem=out_send.at[k], recv_sem=out_recv.at[k],
                 device_id={"grid": peer}, device_id_type=MESH)
             copy.start()
             out_copies.append(copy)
+    for k in range(1, n):
+        for part in range(2):
+            early_copy(part, k).wait()
+        peer = (me + n - k) % n
+        scale = scales_of(band * n + peer)[0]
+        value = scale[0] * packed[0, 0, peer, :early, :]
+        for i in range(1, ITERS + 1):
+            value = value + scale[i] * early_land[peer, i - 1]
+        land[peer, :early, :] = value
     for group in range(GROUPS):
         for kind in range(2):
             for k in range(1, n):
@@ -446,13 +525,13 @@
 
 
 def unpack_kernel(halves, planes, land, coef, out, alphas, betas):
-    owners, cells = land.shape[0], land.shape[3]
+    owners, cells = land.shape[0], land.shape[2]
     upper = lax.broadcasted_iota(jnp.int32, (SUBLANES, cells), 0) < PART
     for owner in range(owners):
         at = slice(owner % halves * SUBLANES, (owner % halves + 1) * SUBLANES)
         for pair in range(planes // 2):
             here = slice(pair * SUBLANES, (pair + 1) * SUBLANES)
-            one, two = land[owner, 0, here, :], land[owner, 1, here, :]
+            one, two = land[owner, here, :], land[owner, slice(here.start + planes * PART, here.stop + planes * PART), :]
             out[0, owner // halves, 0, at, 2 * pair * cells:(2 * pair + 1) * cells] = jnp.where(upper, one, pltpu.roll(two, PART, 0))
             out[0, owner // halves, 0, at, (2 * pair + 1) * cells:(2 * pair + 2) * cells] = jnp.where(upper, pltpu.roll(one, PART, 0), two)
     alphas[0] = coef[0:1, :ITERS]
@@ -483,14 +562,16 @@
     f32, bf16 = jnp.float32, jnp.bfloat16
     dma = pltpu.SemaphoreType.DMA
     members = n * band_n
-    land_shape = (n, GROUPS, piece, cells)
-    start, energies, potential = (pltpu.with_memory_space_constraint(value, pltpu.MemorySpace.HBM) for value in (start, energies, potential))
+    land_shape = (n, GROUPS * piece, cells)
+    operands = (start, energies, sites[:, 0], potential, forward_y, back_y, all_z, x_wide)
+    operands = (pltpu.with_memory_space_constraint(value, pltpu.MemorySpace.HBM) for value in operands)
     land, coef = pl.pallas_call(
         functools.partial(recursion_kernel, (n, band_n, grid_size, halves)),
         out_shape=(jax.ShapeDtypeStruct(land_shape, f32), jax.ShapeDtypeStruct((2, LANES), f32)),
-        in_specs=[hbm, hbm, pl.BlockSpec(memory_space=pltpu.SMEM)] + [hbm] * 5,
+        in_specs=[hbm] * 8,
         out_specs=(vmem, vmem),
         scratch_shapes=[
+            pltpu.SMEM((3,), jnp.int32),
             pltpu.VMEM((half_grid, cells), f32), pltpu.VMEM((grid_size, half_cells), f32), pltpu.VMEM((grid_size, cells), f32),
             pltpu.VMEM((rows, 3 * rows), bf16), pltpu.VMEM(potential.shape, f32),
             pltpu.VMEM((grid_size, cells), f32), pltpu.VMEM((grid_size, cells), f32),
@@ -502,13 +583,14 @@
             pltpu.VMEM((cells, half_cells), bf16), pltpu.VMEM((cells, half_cells), bf16),
             pltpu.VMEM((rows, cells), bf16), pltpu.VMEM((rows, cells), bf16),
             pltpu.VMEM((rows, cells), bf16), pltpu.VMEM((rows, cells), bf16),
-            pltpu.VMEM(land_shape, f32),
-            pltpu.VMEM((2, members, 1, LANES), f32), pltpu.VMEM((2, members, LANES), f32),
-            dma((5,)), dma((2,)), dma((2, GROUPS, n)), dma((2, GROUPS, n)), dma((n,)), dma((n,)),
-            dma((2, members)), dma((2, members)),
+            pltpu.VMEM((2, rows, cells), f32), pltpu.VMEM(land_shape, f32),
+            pltpu.VMEM((n, ITERS, EARLY * piece // 2, cells), f32),
+            pltpu.VMEM((2, members, 1, LANES), f32), pltpu.VMEM((3, members, LANES), f32),
+            dma((6,)), dma((2,)), dma((2, GROUPS, n)), dma((2, GROUPS, n)), dma((n,)), dma((n,)),
+            dma((2, members)), dma((2, members)), pltpu.SemaphoreType.REGULAR, dma((2, n)), dma((2, n)),
         ],
         compiler_params=pltpu.CompilerParams(collective_id=0, has_side_effects=True, vmem_limit_bytes=36 * 1024 * 1024),
-    )(start, energies, sites[:, 0], potential, *(pltpu.with_memory_space_constraint(value, pltpu.MemorySpace.HBM) for value in (forward_y, back_y, all_z, x_wide)))
+    )(*operands)
     scalar = jax.ShapeDtypeStruct((1, 1, ITERS), f32)
     out, alphas, betas = pl.pallas_call(
         functools.partial(unpack_kernel, halves, planes),

time: 60.1 us -> 55.5 us (0.923)
  Pallas kernels: 58.7 us -> 54.8 us
  local copies, waits for them, and re-layouts: 0.65 us -> 0 us
    pallas_call x1, Pallas kernels: 57.6 us -> 53.7 us  [field_body(): pl.pallas_call(functools.partial(recursion_kernel, (n, band_n, grid_size,...]
    unnamed x2 -> x0, local copies, waits for them, and re-layouts: 0.65 us -> none
where the time goes in v1:
time: 55.5 us; the launch traced here: 55.4 us
  Pallas kernels  54.8 us (99%)
  between operations  0.64 us (1%)
    pallas_call x1, Pallas kernels, field_body(): pl.pallas_call(functools.partial(recursion_kernel, (n, band_n, grid_size,...  53.7 us

profile of v1, /device:TPU:1, one launch (start us, length us, event | category | flops | bytes accessed | tf_op | source)
XLA Modules:
  0.0 55.4 jit_solution(8233602323344672710)
XLA Ops:
  0.6 53.7 %shard_map.103 = (f32[8,32,1024]{2,1,0:T(8,128)S(1)}, f32[2,128]{1,0:T(2,128)S(1)}) custom-call(f32[1,4,1,16,4096]{4,3,2,1,0:T(8,128)} %start.1, f32[4,16,4096]{2,1,0:T(8,128)} %energies.1, s32[3]{0:T(128)} %bitcast.1, f32[32,32,32]{2,1,0:T(8,128)} %pot.1, f32[16,1024]{1,0:T(8,128)} %constant.8.clone.forward_y, f32[32,512]{1,0:T(8,128)} %constant.9.clone.back_y, ...), custom_call_target="tpu_custom_call" | custom-call | tf_op jit(solution)/shard_map/pallas_call | solution.py:568
  54.3 1.0 %shard_map.104 = (f32[1,4,1,16,4096]{4,3,2,1,0:T(8,128)}, f32[1,1,4]{2,1,0:T(1,128)}, f32[1,1,4]{2,1,0:T(1,128)}) custom-call(f32[8,32,1024]{2,1,0:T(8,128)S(1)} %get-tuple-element.8.land, f32[2,128]{1,0:T(2,128)S(1)} %get-tuple-element.9.coef), custom_call_target="tpu_custom_call" | custom-call | tf_op jit(solution)/shard_map/pallas_call | solution.py:595

commit v2 on v1

--- a/solution.py
+++ b/solution.py
@@ -122,8 +122,8 @@
 LANES = 128
 SUBLANES = 8
 GROUPS = 2
-EARLY = 1
-FIRST_EIGHTHS = 5
+EARLY_EIGHTHS = (4, 3)
+ORDER = "F0 F1 F2 F3 W0 W1 W2 W3 X0 X1 X2 X3"
 PART = SUBLANES // GROUPS
 
 
@@ -196,7 +196,7 @@
     planes = grid_size // n
     rows = grid_size * PART
     piece = planes * PART
-    early = EARLY * piece // 2
+    early = piece // 2
     quarter = cells // 4
     total_count = float(grid_size * SUBLANES * cells * members)
 
@@ -209,8 +209,7 @@
         for i, (source, target) in enumerate((
             (forward_y, forward_y_here), (back_y, back_y_here), (all_z, all_z_here), (x_far, x_wide), (pot, pot_here), (sites, sites_here)))
     ]
-    for copy in load_copies + table_copies:
-        copy.start()
+    load_copies[0].start()
     barrier = pltpu.get_barrier_semaphore()
     for k in range(1, band_n):
         pl.semaphore_signal(barrier, inc=1, device_id={"band": (band + k) % band_n}, device_id_type=MESH)
@@ -245,14 +244,17 @@
             recv_sem=recv_sem.at[kind, group, k], device_id={"grid": peer}, device_id_type=MESH)
 
     load_copies[0].wait()
+    for copy in load_copies[1:] + table_copies:
+        copy.start()
     pack(0)
+    pl.semaphore_wait(barrier, n + band_n - 2)
+    for k in range(1, n):
+        piece_copy(0, 0, k).start()
     load_copies[1].wait()
     pack(1)
-    pl.semaphore_wait(barrier, n + band_n - 2)
-    for group in range(GROUPS):
-        for kind in range(2):
-            for k in range(1, n):
-                piece_copy(kind, group, k).start()
+    for kind, group in ((1, 0), (0, 1), (1, 1)):
+        for k in range(1, n):
+            piece_copy(kind, group, k).start()
     for k in range(1, band_n):
         pl.semaphore_signal(plane_sem, inc=1, device_id={"band": (band + k) % band_n}, device_id_type=MESH)
     for group in range(GROUPS):
@@ -286,7 +288,6 @@
     for x in range(grid_size):
         site_table[PART * x:PART * (x + 1), :] = jnp.broadcast_to(pot_order[x:x + 1, :], (PART, cells))
 
-    past[...] = jnp.zeros_like(past)
     pl.semaphore_wait(plane_sem, band_n - 1)
 
     quarters = [slice(i * quarter, (i + 1) * quarter) for i in range(4)]
@@ -304,8 +305,9 @@
         high, low = split(value)
         return jnp.dot(x_wide[...], jnp.concatenate([high, high, low], axis=0), preferred_element_type=jnp.float32)
 
-    first_columns = cells * FIRST_EIGHTHS // 8
-    early_columns = (pl.ds(0, first_columns), pl.ds(first_columns, cells - first_columns))
+    eighth = cells // 8
+    early_columns = [pl.ds(sum(EARLY_EIGHTHS[:i]) * eighth, EARLY_EIGHTHS[i] * eighth) for i in range(len(EARLY_EIGHTHS))]
+    early_stop = sum(EARLY_EIGHTHS) * eighth
 
     def early_copy(part, k):
         peer = (me + k) % n
@@ -313,6 +315,10 @@
         return pltpu.make_async_remote_copy(
             src_ref=basis.at[0, pl.ds(1, ITERS), at, early_columns[part]], dst_ref=early_land.at[me, :, :, early_columns[part]],
             send_sem=early_send.at[part, k], recv_sem=early_recv.at[part, k], device_id={"grid": peer}, device_id_type=MESH)
+
+    def send_early(part):
+        for k in range(1, n):
+            early_copy(part, k).start()
 
     def message_copy(stage, k):
         return pltpu.make_async_remote_copy(
@@ -345,66 +351,60 @@
         message = jnp.where(lane_is(place + LANES // 2), alpha, message)
         return alpha, gamma, message
 
-    def step(t, results, final=False):
+    def step(t, results, first=False, final=False):
         alpha, gamma, message = settle(t, results)
         group, j = t // ITERS, t % ITERS
-        before, earlier, now = jnp.maximum(j - 1, 0), jnp.maximum(j - 2, 0), j % 2
         if final:
             send_message(0, message)
+        if first:
+            for k in range(1, n):
+                piece_copy(0, group, k).wait_recv()
+            for at in tiles:
+                spread_quarters(at, [basis[group, 0, at, cols] for cols in quarters])
         else:
-            keep = jnp.where(jnp.full((1, 1), j, jnp.int32) == 0, 0.0, 1.0)
-            alpha, gamma = alpha * keep, gamma * keep
-
-            @pl.when(j == 0)
-            def _():
-                for k in range(1, n):
-                    piece_copy(0, group, k).wait_recv()
-                for at in tiles:
-                    spread_quarters(at, [basis[group, 0, at, cols] for cols in quarters])
+            before, earlier, now = j - 1, jnp.maximum(j - 2, 0), j % 2
 
         def forward(i):
             cols = quarters[i]
             source, depth = (cols, quarter) if i < 2 else (odd, 2 * quarter)
             spectrum = dot3((vec_high[:, source], vec_low[:, source]), (to_high[:depth, cols], to_low[:depth, cols]))
-            spectrum = spectrum - alpha * past[1 - now, :, cols] - gamma * past[now, :, cols]
-            past[now, :, cols] = spectrum
+            if first:
+                past[0, :, cols] = spectrum
+                past[1, :, cols] = jnp.zeros_like(spectrum)
+            else:
+                spectrum = spectrum - alpha * past[1 - now, :, cols] - gamma * past[now, :, cols]
+                past[now, :, cols] = spectrum
             return spectrum
 
         def weigh(i, spectrum):
-            return times_x(spectrum) * site_table[:, quarters[i]]
+            return times_x(past[0 if first else now, :, quarters[i]]) * site_table[:, quarters[i]]
 
         def finish(i, spectrum):
             mid_high[:, quarters[i]], mid_low[:, quarters[i]] = split(times_x(spectrum))
 
-        first, second = forward(0), forward(1)
-        first = weigh(0, first)
-        third = forward(2)
-        second = weigh(1, second)
-        finish(0, first)
-        fourth = forward(3)
-        third = weigh(2, third)
-        finish(1, second)
-        fourth = weigh(3, fourth)
-        finish(2, third)
-        finish(3, fourth)
+        work = {}
+        for name in ORDER.split():
+            i = int(name[1])
+            if name[0] == "F":
+                work[i] = forward(i)
+            elif name[0] == "W":
+                work[i] = weigh(i, work[i])
+            else:
+                finish(i, work[i])
         norm_part = jnp.zeros((SUBLANES, quarter), jnp.float32)
         for at in tiles:
             for cols in quarters:
-                value = basis[group, j, at, cols] - alpha * basis[group, before, at, cols] - gamma * basis[group, earlier, at, cols]
-                basis[group, j, at, cols] = value
+                value = basis[group, j, at, cols]
+                if not first:
+                    value = value - alpha * basis[group, before, at, cols] - gamma * basis[group, earlier, at, cols]
+                    basis[group, j, at, cols] = value
                 norm_part = norm_part + folded(value * value)
         norm = total_of([norm_part])
-        if not final:
-
-            @pl.when(j == 0)
-            def _():
-                for k in range(1, n):
-                    piece_copy(1, group, k).wait_recv()
-
-            @pl.when(t == ITERS)
-            def _():
-                for k in range(1, n):
-                    early_copy(0, k).start()
+        if first:
+            for k in range(1, n):
+                piece_copy(1, group, k).wait_recv()
+            if group == 1:
+                send_early(0)
 
         def back(at, cols):
             return dot3((mid_high[:, at], mid_low[:, at]), (from_high[at, cols], from_low[at, cols]))
@@ -429,10 +429,13 @@
     nothing, no_part = jnp.zeros((1, 1), jnp.float32), jnp.zeros((SUBLANES, quarter), jnp.float32)
     results = (no_part, no_part, nothing, nothing, jnp.zeros((1, LANES), jnp.float32))
     steps = GROUPS * ITERS
-    results = step(steps - 1, lax.fori_loop(0, steps - 1, step, results), True)
+    for group in range(GROUPS):
+        results = step(group * ITERS, results, first=True)
+        stop = (group + 1) * ITERS - (group == GROUPS - 1)
+        results = lax.fori_loop(group * ITERS + 1, stop, step, results)
+    results = step(steps - 1, results, final=True)
     send_message(1, settle(steps, results)[2])
-    for k in range(1, n):
-        early_copy(1, k).start()
+    send_early(1)
 
     def tables_of(stage):
         for k in range(1, members):
@@ -447,72 +450,81 @@
     order = wide_lane % SUBLANES
     used = jnp.logical_and(order <= ITERS, wide_lane < SUBLANES * GROUPS)
 
-    def inner(norms, left, right):
-        return total_of([norms * left * right]) / total_count
-
-    def global_step(tables, vector, previous, beta):
-        norms, diagonal, coupling = tables
+    def image_of(tables, vector):
+        diagonal, coupling = tables[1:]
         raised = jnp.where(order > 0, pltpu.roll(vector, 1, 1), 0.0)
         lowered = jnp.where(order < ITERS, pltpu.roll(coupling * vector, LANES - 1, 1), 0.0)
-        image = jnp.where(used, raised + jnp.where(order < ITERS, diagonal, 0.0) * vector + lowered, 0.0)
-        alpha_now = inner(norms, vector, image)
-        rest = image - alpha_now * vector - beta * previous
-        beta_now = jnp.sqrt(inner(norms, rest, rest))
-        return alpha_now, beta_now, rest / beta_now, vector
+        return jnp.where(used, raised + jnp.where(order < ITERS, diagonal, 0.0) * vector + lowered, 0.0)
 
     alphas, betas = jnp.zeros((1, LANES), jnp.float32), jnp.zeros((1, LANES), jnp.float32)
     tables = tables_of(0)
-    first = jnp.where(jnp.logical_and(used, order == 0), 1.0, 0.0)
-    vector, previous, beta = first / jnp.sqrt(inner(tables[0], first, first)), jnp.zeros((members, LANES), jnp.float32), nothing
+    vector, previous = jnp.where(jnp.logical_and(used, order == 0), 1.0, 0.0), jnp.zeros((members, LANES), jnp.float32)
+    size = nothing
     for j in range(ITERS):
         if j == ITERS - 1:
             tables = tables_of(1)
-        alpha, beta, vector, previous = global_step(tables, vector, previous, beta)
-        alphas, betas = jnp.where(lane == j, alpha, alphas), jnp.where(lane == j, beta, betas)
-    coef[0:1, :] = alphas
-    coef[1:2, :] = betas
+        image = image_of(tables, vector)
+        size_before, size = size, total_of([tables[0] * vector * vector])
+        alpha = total_of([tables[0] * vector * image]) / size
+        rest = image - alpha * vector
+        if j > 0:
+            ratio = size / size_before
+            betas = jnp.where(lane == j - 1, jnp.sqrt(ratio), betas)
+            rest = rest - ratio * previous
+        alphas = jnp.where(lane == j, alpha, alphas)
+        vector, previous = rest, vector
     norms, diagonal, coupling = tables
     top = ITERS - 1
     weights = vector - jnp.where(order == top, diagonal * pltpu.roll(vector, LANES - 1, 1), 0.0)
     weights = weights - jnp.where(order == top - 1, pltpu.roll(coupling, LANES - 1, 1) * pltpu.roll(vector, LANES - 2, 1), 0.0)
+    size_before, size = size, total_of([norms * vector * vector])
+    unit = 1.0 / jnp.sqrt(size / total_count)
+    coef[0:1, :] = alphas
+    coef[1:2, :] = jnp.where(lane == ITERS - 1, jnp.sqrt(size / size_before), betas)
     gathered[2] = weights
 
     def scales_of(owner):
         row = gathered[2, pl.ds(owner, 1), :]
         return [
-            [jnp.sum(jnp.where(lane == SUBLANES * group + i, row, 0.0), axis=1, keepdims=True) for i in range(ITERS + 1)]
+            [jnp.sum(jnp.where(lane == SUBLANES * group + i, row, 0.0), axis=1, keepdims=True) * unit for i in range(ITERS + 1)]
             for group in range(GROUPS)
         ]
 
     scales = scales_of(rank)
+
+    def own_value(group, at, cols):
+        return sum((scales[group][i] * basis[group, i, at, cols] for i in range(1, ITERS + 1)), scales[group][0] * basis[group, 0, at, cols])
+
+    every, late = slice(0, cells), slice(early_stop, cells)
     out_copies = []
     for k in range(1, n + 1):
         peer = (me + k) % n
-        for group in range(GROUPS):
-            skip = early if group == 0 and k < n else 0
-            at = pl.ds(pl.multiple_of(peer * piece + skip, SUBLANES), piece - skip)
-            value = sum((scales[group][i] * basis[group, i, at, :] for i in range(1, ITERS + 1)), scales[group][0] * basis[group, 0, at, :])
-            target = slice(group * piece + skip, (group + 1) * piece)
-            if k < n:
-                outgoing[peer, target, :] = value
-            else:
-                land[me, target, :] = value
-        if k < n:
-            sent = pl.ds(early, GROUPS * piece - early)
+        here = pl.multiple_of(peer * piece, piece)
+        target, place = (outgoing, peer) if k < n else (land, me)
+        target[place, early:piece, :] = own_value(0, pl.ds(here + early, piece - early), every)
+        target[place, piece:, :] = own_value(1, pl.ds(here, piece), every)
+        if k == n:
+            target[place, :early, :] = own_value(0, pl.ds(here, early), every)
+            continue
+        areas = [(pl.ds(early, GROUPS * piece - early), pl.ds(0, cells))]
+        if early_stop < cells:
+            target[place, :early, late] = own_value(0, pl.ds(here, early), late)
+            areas.append((pl.ds(0, early), pl.ds(early_stop, cells - early_stop)))
+        for i, (at, cols) in enumerate(areas):
             copy = pltpu.make_async_remote_copy(
-                src_ref=outgoing.at[peer, sent, :], dst_ref=land.at[me, sent, :], send_sem=out_send.at[k], recv_sem=out_recv.at[k],
+                src_ref=outgoing.at[peer, at, cols], dst_ref=land.at[me, at, cols], send_sem=out_send.at[i, k], recv_sem=out_recv.at[i, k],
                 device_id={"grid": peer}, device_id_type=MESH)
             copy.start()
             out_copies.append(copy)
     for k in range(1, n):
-        for part in range(2):
+        for part in range(len(EARLY_EIGHTHS)):
             early_copy(part, k).wait()
         peer = (me + n - k) % n
         scale = scales_of(band * n + peer)[0]
-        value = scale[0] * packed[0, 0, peer, :early, :]
+        value = scale[0] * packed[0, 0, peer, :early, :early_stop]
         for i in range(1, ITERS + 1):
-            value = value + scale[i] * early_land[peer, i - 1]
-        land[peer, :early, :] = value
+            value = value + scale[i] * early_land[peer, i - 1, :, :early_stop]
+        land[peer, :early, :early_stop] = value
     for group in range(GROUPS):
         for kind in range(2):
             for k in range(1, n):
@@ -584,10 +596,10 @@
             pltpu.VMEM((rows, cells), bf16), pltpu.VMEM((rows, cells), bf16),
             pltpu.VMEM((rows, cells), bf16), pltpu.VMEM((rows, cells), bf16),
             pltpu.VMEM((2, rows, cells), f32), pltpu.VMEM(land_shape, f32),
-            pltpu.VMEM((n, ITERS, EARLY * piece // 2, cells), f32),
+            pltpu.VMEM((n, ITERS, piece // 2, cells), f32),
             pltpu.VMEM((2, members, 1, LANES), f32), pltpu.VMEM((3, members, LANES), f32),
-            dma((6,)), dma((2,)), dma((2, GROUPS, n)), dma((2, GROUPS, n)), dma((n,)), dma((n,)),
-            dma((2, members)), dma((2, members)), pltpu.SemaphoreType.REGULAR, dma((2, n)), dma((2, n)),
+            dma((6,)), dma((2,)), dma((2, GROUPS, n)), dma((2, GROUPS, n)), dma((2, n)), dma((2, n)),
+            dma((2, members)), dma((2, members)), pltpu.SemaphoreType.REGULAR, dma((len(EARLY_EIGHTHS), n)), dma((len(EARLY_EIGHTHS), n)),
         ],
         compiler_params=pltpu.CompilerParams(collective_id=0, has_side_effects=True, vmem_limit_bytes=36 * 1024 * 1024),
     )(*operands)

time: 55.5 us -> 54.3 us (0.978)
  Pallas kernels: 54.8 us -> 53.5 us
    pallas_call x1, Pallas kernels: 53.7 us -> 52.4 us  [field_body(): pl.pallas_call(functools.partial(recursion_kernel, (n, band_n, grid_size,...]
where the time goes in v2:
time: 54.3 us; the launch traced here: 54.1 us
  Pallas kernels  53.5 us (99%)
  between operations  0.64 us (1%)
    pallas_call x1, Pallas kernels, field_body(): pl.pallas_call(functools.partial(recursion_kernel, (n, band_n, grid_size,...  52.4 us

profile of v2, /device:TPU:1, one launch (start us, length us, event | category | flops | bytes accessed | tf_op | source)
XLA Modules:
  0.0 54.1 jit_solution(14619539471037044515)
XLA Ops:
  0.6 52.4 %shard_map.103 = (f32[8,32,1024]{2,1,0:T(8,128)S(1)}, f32[2,128]{1,0:T(2,128)S(1)}) custom-call(f32[1,4,1,16,4096]{4,3,2,1,0:T(8,128)} %start.1, f32[4,16,4096]{2,1,0:T(8,128)} %energies.1, s32[3]{0:T(128)} %bitcast.1, f32[32,32,32]{2,1,0:T(8,128)} %pot.1, f32[16,1024]{1,0:T(8,128)} %constant.8.clone.forward_y, f32[32,512]{1,0:T(8,128)} %constant.9.clone.back_y, ...), custom_call_target="tpu_custom_call" | custom-call | tf_op jit(solution)/shard_map/pallas_call | solution.py:580
  53.1 1.0 %shard_map.104 = (f32[1,4,1,16,4096]{4,3,2,1,0:T(8,128)}, f32[1,1,4]{2,1,0:T(1,128)}, f32[1,1,4]{2,1,0:T(1,128)}) custom-call(f32[8,32,1024]{2,1,0:T(8,128)S(1)} %get-tuple-element.8.land, f32[2,128]{1,0:T(2,128)S(1)} %get-tuple-element.9.coef), custom_call_target="tpu_custom_call" | custom-call | tf_op jit(solution)/shard_map/pallas_call | solution.py:607

commit v3 on v2

--- a/solution.py
+++ b/solution.py
@@ -123,7 +123,6 @@
 SUBLANES = 8
 GROUPS = 2
 EARLY_EIGHTHS = (4, 3)
-ORDER = "F0 F1 F2 F3 W0 W1 W2 W3 X0 X1 X2 X3"
 PART = SUBLANES // GROUPS
 
 
@@ -382,15 +381,10 @@
         def finish(i, spectrum):
             mid_high[:, quarters[i]], mid_low[:, quarters[i]] = split(times_x(spectrum))
 
-        work = {}
-        for name in ORDER.split():
-            i = int(name[1])
-            if name[0] == "F":
-                work[i] = forward(i)
-            elif name[0] == "W":
-                work[i] = weigh(i, work[i])
-            else:
-                finish(i, work[i])
+        work = [forward(i) for i in range(4)]
+        work = [weigh(i, work[i]) for i in range(4)]
+        for i in range(4):
+            finish(i, work[i])
         norm_part = jnp.zeros((SUBLANES, quarter), jnp.float32)
         for at in tiles:
             for cols in quarters:

time: 54.3 us -> 54.3 us (level)
  no operation moved by 1% of the time
where the time goes in v3:
time: 54.3 us; the launch traced here: 54.1 us
  Pallas kernels  53.5 us (99%)
  between operations  0.64 us (1%)
    pallas_call x1, Pallas kernels, field_body(): pl.pallas_call(functools.partial(recursion_kernel, (n, band_n, grid_size,...  52.4 us

profile of v3, /device:TPU:1, one launch (start us, length us, event | category | flops | bytes accessed | tf_op | source)
XLA Modules:
  0.0 54.1 jit_solution(14619539471037044515)
XLA Ops:
  0.6 52.4 %shard_map.103 = (f32[8,32,1024]{2,1,0:T(8,128)S(1)}, f32[2,128]{1,0:T(2,128)S(1)}) custom-call(f32[1,4,1,16,4096]{4,3,2,1,0:T(8,128)} %start.1, f32[4,16,4096]{2,1,0:T(8,128)} %energies.1, s32[3]{0:T(128)} %bitcast.1, f32[32,32,32]{2,1,0:T(8,128)} %pot.1, f32[16,1024]{1,0:T(8,128)} %constant.8.clone.forward_y, f32[32,512]{1,0:T(8,128)} %constant.9.clone.back_y, ...), custom_call_target="tpu_custom_call" | custom-call | tf_op jit(solution)/shard_map/pallas_call | solution.py:574
  53.1 1.0 %shard_map.104 = (f32[1,4,1,16,4096]{4,3,2,1,0:T(8,128)}, f32[1,1,4]{2,1,0:T(1,128)}, f32[1,1,4]{2,1,0:T(1,128)}) custom-call(f32[8,32,1024]{2,1,0:T(8,128)S(1)} %get-tuple-element.8.land, f32[2,128]{1,0:T(2,128)S(1)} %get-tuple-element.9.coef), custom_call_target="tpu_custom_call" | custom-call | tf_op jit(solution)/shard_map/pallas_call | solution.py:601

commit v4 on v3

--- a/solution.py
+++ b/solution.py
@@ -353,8 +353,6 @@
     def step(t, results, first=False, final=False):
         alpha, gamma, message = settle(t, results)
         group, j = t // ITERS, t % ITERS
-        if final:
-            send_message(0, message)
         if first:
             for k in range(1, n):
                 piece_copy(0, group, k).wait_recv()
@@ -382,6 +380,8 @@
             mid_high[:, quarters[i]], mid_low[:, quarters[i]] = split(times_x(spectrum))
 
         work = [forward(i) for i in range(4)]
+        if final:
+            send_message(0, message)
         work = [weigh(i, work[i]) for i in range(4)]
         for i in range(4):
             finish(i, work[i])
@@ -491,7 +491,7 @@
 
     every, late = slice(0, cells), slice(early_stop, cells)
     out_copies = []
-    for k in range(1, n + 1):
+    for k in [*range(n // 2 - 1, 0, -1), *range(n // 2, n + 1)]:
         peer = (me + k) % n
         here = pl.multiple_of(peer * piece, piece)
         target, place = (outgoing, peer) if k < n else (land, me)

time: 54.3 us -> 54.3 us (level)
  no operation moved by 1% of the time
where the time goes in v4:
time: 54.3 us; the launch traced here: 54.1 us
  Pallas kernels  53.5 us (99%)
  between operations  0.64 us (1%)
    pallas_call x1, Pallas kernels, field_body(): pl.pallas_call(functools.partial(recursion_kernel, (n, band_n, grid_size,...  52.4 us

profile of v4, /device:TPU:1, one launch (start us, length us, event | category | flops | bytes accessed | tf_op | source)
XLA Modules:
  0.0 54.1 jit_solution(5010498458166056770)
XLA Ops:
  0.6 52.4 %shard_map.103 = (f32[8,32,1024]{2,1,0:T(8,128)S(1)}, f32[2,128]{1,0:T(2,128)S(1)}) custom-call(f32[1,4,1,16,4096]{4,3,2,1,0:T(8,128)} %start.1, f32[4,16,4096]{2,1,0:T(8,128)} %energies.1, s32[3]{0:T(128)} %bitcast.1, f32[32,32,32]{2,1,0:T(8,128)} %pot.1, f32[16,1024]{1,0:T(8,128)} %constant.8.clone.forward_y, f32[32,512]{1,0:T(8,128)} %constant.9.clone.back_y, ...), custom_call_target="tpu_custom_call" | custom-call | tf_op jit(solution)/shard_map/pallas_call | solution.py:574
  53.1 1.0 %shard_map.104 = (f32[1,4,1,16,4096]{4,3,2,1,0:T(8,128)}, f32[1,1,4]{2,1,0:T(1,128)}, f32[1,1,4]{2,1,0:T(1,128)}) custom-call(f32[8,32,1024]{2,1,0:T(8,128)S(1)} %get-tuple-element.8.land, f32[2,128]{1,0:T(2,128)S(1)} %get-tuple-element.9.coef), custom_call_target="tpu_custom_call" | custom-call | tf_op jit(solution)/shard_map/pallas_call | solution.py:601
